TPU v7x, 32 devices: a whole 2x2x4 slice. The times are simulated.
32 devices in a mesh: tm: 4 (over y, x), rows: 2 (over core), batch: 4 (over z).
Axes of the slice: x: 2, y: 2, z: 4, core: 2. Of those that a mesh axis runs over, the one named last changes fastest.
Arguments:
- inputs: bfloat16 [4, 8, 16, 128, 384], P('batch', 'tm', 'rows'), parts along dimension 0, may hold values from -16 to 16
- norm_gain: float32 [384], replicated, may hold values from 0.1 to 1.9
- norm_bias: float32 [384], replicated, may hold values from -3 to 3
- conv_weight: bfloat16 [3, 3, 3, 384, 384], replicated, may hold values from -0.0625 to 0.0625
- conv_bias: float32 [384], replicated, may hold values from -2 to 2
Outputs:
- decoded: bfloat16 [4, 8, 16, 128, 384], P('batch', 'tm', 'rows'), parts along dimension 0
There are 4 independent parts, one for each index of `batch`. A program takes and returns all parts, laid end to end along the dimension named above; an argument that names none is the same for every part. Nothing has to cross between parts.
All inputs are finite; a program needn't handle non-finite values.
Results may differ from a plain program's by a relative error of at most 0.0025.
Values may be sent and summed in bfloat16 or wider, within the bound.
No kernel may reach another device: no remote copies, remote signals or barrier semaphores. Data moves between devices by JAX's collectives and lax.ppermute only.
A program may use at most 128 MiB of HBM per device.

v0:
```python
import jax
import jax.numpy as jnp
from jax import lax
from jax.sharding import PartitionSpec as P

GROUPS = 32


epsilon = 1e-06


def from_behind(value, axis, steps):
    count = lax.axis_size(axis)
    initial, last = (max(0, -steps), min(count, count - steps))
    return lax.ppermute(value, axis, [(source, source + steps) for source in range(initial, last)])


def with_halo(block, sides, width):
    for axis, dim in sides:
        count = lax.axis_size(axis)
        forward = [(i, i + 1) for i in range(count - 1)]
        backward = [(target, source) for source, target in forward]
        low = lax.ppermute(
            lax.slice_in_dim(block, block.shape[dim] - width, None, axis=dim), axis, forward
        )
        high = lax.ppermute(lax.slice_in_dim(block, 0, width, axis=dim), axis, backward)
        block = jnp.concatenate([low, block, high], axis=dim)
    return block


def convolve(padded, conv_weight, frames, height, width_dev):
    channels = padded.shape[-1]
    summed = jnp.zeros(
        (padded.shape[0] * frames * height * width_dev, conv_weight.shape[-1]), jnp.float32
    )
    for tap_time in range(3):
        for tap_row in range(3):
            slab_rows = padded[:, tap_time : tap_time + frames, tap_row : tap_row + height]
            columns = jnp.concatenate(
                [
                    slab_rows[:, :, :, 0:width_dev],
                    slab_rows[:, :, :, 1 : width_dev + 1],
                    slab_rows[:, :, :, 2 : width_dev + 2],
                ],
                axis=-1,
            )
            kernel = conv_weight[tap_time, tap_row].reshape(3 * channels, -1)
            summed = summed + jnp.dot(
                columns.reshape(-1, 3 * channels), kernel, preferred_element_type=jnp.float32
            )
    return summed


def grouped(chan_values, per_group):
    return jnp.sum(chan_values.reshape(-1, per_group), axis=1)


def shards(inputs, norm_gain, norm_bias, conv_weight, conv_bias):
    values = inputs.astype(jnp.float32)
    clip_count, frames, height, width_dev, channels = inputs.shape
    per_group = channels // GROUPS
    cell_count = (
        1.0
        * clip_count
        * frames
        * height
        * width_dev
        * per_group
        * lax.axis_size("tm")
        * lax.axis_size("rows")
    )
    chan_sum = jnp.sum(values, axis=(0, 1, 2, 3))
    chan_raw = jnp.sum(values * values, axis=(0, 1, 2, 3))
    total_sum, total_square = lax.psum(
        (grouped(chan_sum, per_group), grouped(chan_raw, per_group)), ("tm", "rows")
    )
    group_mean = total_sum / cell_count
    group_var = total_square / cell_count - group_mean * group_mean
    centered = values - jnp.repeat(group_mean, per_group)
    inverse = jnp.repeat(lax.rsqrt(group_var + epsilon), per_group)
    normed = centered * inverse * norm_gain + norm_bias
    active = (normed * jax.nn.sigmoid(normed)).astype(jnp.bfloat16)
    earlier = from_behind(active, "tm", 1)
    extended = with_halo(jnp.concatenate([earlier, active], axis=1), (("rows", 2),), 1)
    padded = jnp.pad(extended, ((0, 0), (0, 0), (0, 0), (1, 1), (0, 0)))
    summed = convolve(padded, conv_weight, frames, height, width_dev)
    result = values + summed.reshape(values.shape) + conv_bias
    return result.astype(jnp.bfloat16)


def solution(mesh):
    placed = (P("batch", "tm", "rows", None, None), P(), P(), P(), P())
    return jax.shard_map(
        shards,
        mesh=mesh,
        in_specs=placed,
        out_specs=P("batch", "tm", "rows", None, None),
        check_vma=False,
    )
```

profile of v0, /device:TPU:29, one launch (start us, length us, event | category | flops | bytes accessed | tf_op | source)
XLA Modules:
  0.0 139.0 jit_solution(7587805098458186710)
XLA Ops:
  0.0 1.9 %convert_reduce_fusion = (f32[384]{0:T(512)S(1)}, f32[384]{0:T(512)S(1)}) fusion(bf16[1,2,8,128,384]{4,3,2,1,0:T(8,128)(2,1)} %param.5), kind=kLoop, calls=%fused_computation.6 | loop fusion | flops 3144960 | bytes 1575936 | tf_op jit(solution)/shard_map/reduce_sum | solution.py:72
  1.9 0.1 reshape.51
  2.0 0.1 reshape.52
  2.1 0.1 reduce_sum.37
  2.2 0.1 reduce_sum.39
  2.3 11.8 %all-reduce.1 = (f32[32]{0:T(128)S(1)}, f32[32]{0:T(128)S(1)}) all-reduce(f32[32]{0:T(128)S(1)} %reduce_sum.39, f32[32]{0:T(128)S(1)} %reduce_sum.37), channel_id=1, replica_groups=mesh['tm'=4,'rows'=2,'batch'=4] {'tm','rows'}, use_global_device_ids=true, to_apply=%region_5.0 | all-reduce | flops 64 | bytes 512 | tf_op jit(solution)/shard_map/psum | solution.py:74
  14.2 0.1 broadcast_in_dim.10
  14.3 0.1 mul.29
  14.4 0.1 broadcast_in_dim.4
  14.4 0.1 sub.13
  14.5 2.5 %fusion.14 = bf16[1,2,8,128,384]{4,3,2,1,0:T(8,128)(2,1)S(1)} fusion(bf16[1,2,8,128,384]{4,3,2,1,0:T(8,128)(2,1)} %param.5, f32[384]{0:T(512)} %param.7, f32[384]{0:T(512)} %param.6, f32[384]{0:T(512)S(1)} %mul.29, f32[384]{0:T(512)S(1)} %sub.13), kind=kLoop, calls=%fused_computation.33 | loop fusion | flops 7864320 | bytes 3151872 | tf_op jit(solution)/shard_map/convert_element_type | solution.py:82
  17.1 2.5 %collective-permute-start = (bf16[1,2,8,128,384]{4,3,2,1,0:T(8,128)(2,1)S(1)}, bf16[1,2,8,128,384]{4,3,2,1,0:T(8,128)(2,1)S(1)}, u32[]{:S(2)}, u32[]{:S(2)}) collective-permute-start(bf16[1,2,8,128,384]{4,3,2,1,0:T(8,128)(2,1)S(1)} %fusion.14), channel_id=1, source_target_pairs={{0,8},{8,16},{16,24},{1,9},{9,17},{17,25},{2,10},{10,18},{18,26},{... | collective-permute-start | bytes 4718600 | tf_op jit(solution)/shard_map/ppermute | solution.py:15
  19.6 34.7 %collective-permute-done = bf16[1,2,8,128,384]{4,3,2,1,0:T(8,128)(2,1)S(1)} collective-permute-done((bf16[1,2,8,128,384]{4,3,2,1,0:T(8,128)(2,1)S(1)}, bf16[1,2,8,128,384]{4,3,2,1,0:T(8,128)(2,1)S(1)}, u32[]{:S(2)}, u32[]{:S(2)}) %collective-permute-start) | collective-permute-done | bytes 1572896 | tf_op jit(solution)/shard_map/ppermute | solution.py:15
  54.3 0.1 pad_maximum_fusion.11
  54.4 1.3 collective-permute-start.1
  55.7 4.5 %collective-permute-start.2 = (bf16[1,4,1,128,384]{4,3,2,1,0:T(8,128)(2,1)S(1)}, bf16[1,4,1,128,384]{4,3,2,1,0:T(8,128)(2,1)S(1)}, u32[]{:S(2)}, u32[]{:S(2)}) collective-permute-start(bf16[1,4,1,128,384]{4,3,2,1,0:T(8,128)(2,1)S(1)} %get-tuple-element.45), channel_id=1, source_target_pairs={{4,0},{5,1},{6,2},{7,3},{12,8},{13,9},{14,10},{15,11},{20,16},{21,... | collective-permute-start | bytes 1179656 | tf_op jit(solution)/shard_map/ppermute | solution.py:26
  60.2 5.8 %fusion.18 = (bf16[1,1,3,384,384]{4,3,2,1,0:T(8,128)(2,1)}, bf16[1,1,3,384,384]{4,3,2,1,0:T(8,128)(2,1)}, bf16[1,1,3,384,384]{4,3,2,1,0:T(8,128)(2,1)}, bf16[1,1...) fusion(bf16[3,3,3,384,384]{4,3,2,1,0:T(8,128)(2,1)} %param.8), kind=kLoop, calls=%fused_computation.42 | loop fusion | bytes 15925248 | tf_op jit(solution)/shard_map/slice | solution.py:47
  66.0 1.9 %select_maximum_fusion = bf16[1,4,10,130,384]{4,3,2,1,0:T(8,128)(2,1)S(1)} fusion(bf16[1,4,1,128,384]{4,3,2,1,0:T(8,128)(2,1)S(1)} %collective-permute-done.2, bf16[1,4,1,128,384]{4,3,2,1,0:T(8,128)(2,1)S(1)} %collective-permute-done.1, bf16[1,2,8,128,384]{4,3,2,1,0:T(8,128)(2,1)S(1)} %fusion.14, bf16[1,2,8,128,384]{4,3,2,1,0:T(8,128)(2,1)S(1)} %collective-permute-done), kind=kLoop, calls=%fused_computation.18 | loop fusion | flops 29952000 | bytes 7925760 | tf_op jit(solution)/shard_map/concatenate | solution.py:27
  67.9 10.3 %fusion.19 = (bf16[1,2,8,128,384]{4,3,2,1,0:T(8,128)(2,1)S(1)}, bf16[1,2,8,128,384]{4,3,2,1,0:T(8,128)(2,1)S(1)}, bf16[1,2,8,128,384]{4,3,2,1,0:T(8,128)(2,1)S(1...) fusion(bf16[1,4,10,130,384]{4,3,2,1,0:T(8,128)(2,1)S(1)} %selec, ...), kind=kLoop, calls=%fused_computation.43 | loop fusion | bytes 56623104 | tf_op jit(solution)/shard_map/slice | solution.py:41
  78.1 1.1 pad_maximum_fusion.9
  79.3 1.1 fusion.20
  80.4 0.3 copy-done.11
  80.7 0.5 copy-done.12
  81.1 0.7 pad_maximum_fusion.1
  81.8 0.5 copy-done.25
  82.3 4.5 %fusion.22 = f32[2048,384]{1,0:T(8,128)} fusion(bf16[2048,1152]{1,0:T(8,128)(2,1)S(1)} %bitcast.42, bf16[1152,384]{1,0:T(8,128)(2,1)S(1)} %bitcast.55), kind=kOutput, calls=%fused_computation.46 | convolution fusion | flops 1811939328 | bytes 8749056 | tf_op jit(solution)/shard_map/dot_general | solution.py:48
  86.8 0.7 pad_maximum_fusion.3
  87.5 0.5 copy-done.24
  88.0 4.6 %fusion.24 = f32[2048,384]{1,0:T(8,128)} fusion(bf16[2048,1152]{1,0:T(8,128)(2,1)S(1)} %bitcast.43, bf16[1152,384]{1,0:T(8,128)(2,1)S(1)} %bitcast.54), kind=kOutput, calls=%fused_computation.48 | convolution fusion | flops 1811939328 | bytes 8749056 | tf_op jit(solution)/shard_map/dot_general | solution.py:48
  92.6 0.9 pad_maximum_fusion.4
  93.5 0.3 copy-done.23
  93.8 4.5 %fusion.25 = f32[2048,384]{1,0:T(8,128)} fusion(bf16[2048,1152]{1,0:T(8,128)(2,1)S(1)} %bitcast.44, bf16[1152,384]{1,0:T(8,128)(2,1)S(1)} %bitcast.53), kind=kOutput, calls=%fused_computation.49 | convolution fusion | flops 1811939328 | bytes 8749056 | tf_op jit(solution)/shard_map/dot_general | solution.py:48
  98.2 0.7 pad_maximum_fusion.5
  98.9 0.5 copy-done.22
  99.4 4.6 %fusion.27 = f32[2048,384]{1,0:T(8,128)} fusion(bf16[2048,1152]{1,0:T(8,128)(2,1)S(1)} %bitcast.45, bf16[1152,384]{1,0:T(8,128)(2,1)S(1)} %bitcast.52), kind=kOutput, calls=%fused_computation.51 | convolution fusion | flops 1811939328 | bytes 8749056 | tf_op jit(solution)/shard_map/dot_general | solution.py:48
  104.0 0.7 pad_maximum_fusion.6
  104.7 0.5 copy-done.21
  105.2 4.5 %fusion.28 = f32[2048,384]{1,0:T(8,128)} fusion(bf16[2048,1152]{1,0:T(8,128)(2,1)S(1)} %bitcast.46, bf16[1152,384]{1,0:T(8,128)(2,1)S(1)} %bitcast.51), kind=kOutput, calls=%fused_computation.52 | convolution fusion | flops 1811939328 | bytes 8749056 | tf_op jit(solution)/shard_map/dot_general | solution.py:48
  109.7 3.2 %pad_maximum_fusion.2 = (bf16[1,2,8,128,1152]{4,3,2,1,0:T(8,128)(2,1)S(1)}, bf16[1,2,8,128,1152]{4,3,2,1,0:T(8,128)(2,1)}, bf16[1,2,8,128,1152]{4,3,2,1,0:T(8,128)(2,1)S(1)}) fusion(bf16[1,2,8,128,384]{4,3,2,1,0:T(8,128)(2,1)S(1)} %copy-done.1, bf16[1,2,8,128,384]{4,3,2,1,0:T(8,128)(2,1)S(1)} %collective-permute-done, ...), kind=kLoop, calls=%fused_computation.11 | loop fusion | flops 47185920 | bytes 26738688 | tf_op jit(solution)/shard_map/concatenate | solution.py:39
  112.9 4.5 %fusion.23 = f32[2048,384]{1,0:T(8,128)} fusion(bf16[2048,1152]{1,0:T(8,128)(2,1)S(1)} %bitcast.41, bf16[1152,384]{1,0:T(8,128)(2,1)S(1)} %bitcast.50), kind=kOutput, calls=%fused_computation.47 | convolution fusion | flops 1811939328 | bytes 8749056 | tf_op jit(solution)/shard_map/dot_general | solution.py:48
  117.4 4.5 %fusion.26 = f32[2048,384]{1,0:T(8,128)} fusion(bf16[2048,1152]{1,0:T(8,128)(2,1)S(1)} %bitcast.40, bf16[1152,384]{1,0:T(8,128)(2,1)S(1)} %bitcast.49), kind=kOutput, calls=%fused_computation.50 | convolution fusion | flops 1811939328 | bytes 8749056 | tf_op jit(solution)/shard_map/dot_general | solution.py:48
  121.9 4.5 %fusion.29 = f32[2048,384]{1,0:T(8,128)} fusion(bf16[2048,1152]{1,0:T(8,128)(2,1)S(1)} %bitcast.39, bf16[1152,384]{1,0:T(8,128)(2,1)S(1)} %bitcast.48), kind=kOutput, calls=%fused_computation.53 | convolution fusion | flops 1811939328 | bytes 8749056 | tf_op jit(solution)/shard_map/dot_general | solution.py:48
  126.4 0.7 pad_maximum_fusion.8
  127.1 0.5 copy-done.14
  127.6 1.0 copy-done.15
  128.6 1.0 copy-done.16
  129.5 7.7 %add_add_fusion = f32[2048,384]{1,0:T(8,128)S(1)} fusion(f32[2048,384]{1,0:T(8,128)} %fusion.29, f32[2048,384]{1,0:T(8,128)} %fusion.28, f32[2048,384]{1,0:T(8,128)} %fusion.27, f32[2048,384]{1,0:T(8,128)} %fusion.26, f32[2048,384]{1,0:T(8,128)S(1)} %copy-done.17, f32[2048,384]{1,0:T(8,128)S(1)} %copy-done.16, f32[2048,384]{1,0:T(8,128)S(1)} %copy-done.15, ...), kind=kOutput, calls=%fused_computation.37 | convolution fusion | flops 1818230784 | bytes 33914880 | tf_op jit(solution)/shard_map/dot_general | solution.py:48
  137.3 1.7 %fusion.17 = bf16[1,2,8,128,384]{4,3,2,1,0:T(8,128)(2,1)} fusion(f32[1,2,8,128,384]{4,3,2,1,0:T(8,128)S(1)} %bitcast.38, bf16[1,2,8,128,384]{4,3,2,1,0:T(8,128)(2,1)S(1)} %copy-done, f32[384]{0:T(512)S(1)} %copy-done.26), kind=kLoop, calls=%fused_computation.36 | loop fusion | flops 3145728 | bytes 6292992 | tf_op jit(solution)/shard_map/convert_element_type | solution.py:88
  (47 shorter events, 0.1 us)
Async XLA Ops:
  17.1 37.2 %collective-permute-start = (bf16[1,2,8,128,384]{4,3,2,1,0:T(8,128)(2,1)S(1)}, bf16[1,2,8,128,384]{4,3,2,1,0:T(8,128)(2,1)S(1)}, u32[]{:S(2)}, u32[]{:S(2)}) collective-permute-start(bf16[1,2,8,128,384]{4,3,2,1,0:T(8,128)(2,1)S(1)} %fusion.14), channel_id=1, source_target_pairs={{0,8},{8,16},{16,24},{1,9},{9,17},{17,25},{2,10},{10,18},{18,26},{... | collective-permute-start | bytes 4718600 | tf_op jit(solution)/shard_map/ppermute | solution.py:15
  54.4 11.6 %collective-permute-start.1 = (bf16[1,4,1,128,384]{4,3,2,1,0:T(8,128)(2,1)S(1)}, bf16[1,4,1,128,384]{4,3,2,1,0:T(8,128)(2,1)S(1)}, u32[]{:S(2)}, u32[]{:S(2)}) collective-permute-start(bf16[1,4,1,128,384]{4,3,2,1,0:T(8,128)(2,1)S(1)} %get-tuple-element.44), channel_id=1, source_target_pairs={{0,4},{1,5},{2,6},{3,7},{8,12},{9,13},{10,14},{11,15},{16,20},{17,... | collective-permute-start | bytes 1179656 | tf_op jit(solution)/shard_map/ppermute | solution.py:23
  55.7 10.3 %collective-permute-start.2 = (bf16[1,4,1,128,384]{4,3,2,1,0:T(8,128)(2,1)S(1)}, bf16[1,4,1,128,384]{4,3,2,1,0:T(8,128)(2,1)S(1)}, u32[]{:S(2)}, u32[]{:S(2)}) collective-permute-start(bf16[1,4,1,128,384]{4,3,2,1,0:T(8,128)(2,1)S(1)} %get-tuple-element.45), channel_id=1, source_target_pairs={{4,0},{5,1},{6,2},{7,3},{12,8},{13,9},{14,10},{15,11},{20,16},{21,... | collective-permute-start | bytes 1179656 | tf_op jit(solution)/shard_map/ppermute | solution.py:26
  79.2 1.4 %copy-start.11 = (bf16[1,2,8,128,384]{4,3,2,1,0:T(8,128)(2,1)S(1)}, bf16[1,2,8,128,384]{4,3,2,1,0:T(8,128)(2,1)}, u32[]{:S(2)}) copy-start(bf16[1,2,8,128,384]{4,3,2,1,0:T(8,128)(2,1)} %get-tuple-element.33) | copy-start | bytes 4718596
  79.3 1.9 %copy-start.12 = (bf16[1,2,8,128,384]{4,3,2,1,0:T(8,128)(2,1)S(1)}, bf16[1,2,8,128,384]{4,3,2,1,0:T(8,128)(2,1)}, u32[]{:S(2)}) copy-start(bf16[1,2,8,128,384]{4,3,2,1,0:T(8,128)(2,1)} %get-tuple-element.34) | copy-start | bytes 4718596
  81.1 1.2 copy-start.25
  82.3 4.5 %copy-start.9 = (bf16[1,2,8,128,384]{4,3,2,1,0:T(8,128)(2,1)S(1)}, bf16[1,2,8,128,384]{4,3,2,1,0:T(8,128)(2,1)}, u32[]{:S(2)}) copy-start(bf16[1,2,8,128,384]{4,3,2,1,0:T(8,128)(2,1)} %get-tuple-element.29) | copy-start | bytes 4718596
  82.3 4.5 %copy-start.10 = (bf16[1,2,8,128,384]{4,3,2,1,0:T(8,128)(2,1)S(1)}, bf16[1,2,8,128,384]{4,3,2,1,0:T(8,128)(2,1)}, u32[]{:S(2)}) copy-start(bf16[1,2,8,128,384]{4,3,2,1,0:T(8,128)(2,1)} %get-tuple-element.30) | copy-start | bytes 4718596
  86.8 1.2 copy-start.24
  88.0 4.6 %copy-start.7 = (bf16[1,2,8,128,384]{4,3,2,1,0:T(8,128)(2,1)S(1)}, bf16[1,2,8,128,384]{4,3,2,1,0:T(8,128)(2,1)}, u32[]{:S(2)}) copy-start(bf16[1,2,8,128,384]{4,3,2,1,0:T(8,128)(2,1)} %get-tuple-element.27) | copy-start | bytes 4718596
  88.0 4.6 %copy-start.8 = (bf16[1,2,8,128,384]{4,3,2,1,0:T(8,128)(2,1)S(1)}, bf16[1,2,8,128,384]{4,3,2,1,0:T(8,128)(2,1)}, u32[]{:S(2)}) copy-start(bf16[1,2,8,128,384]{4,3,2,1,0:T(8,128)(2,1)} %get-tuple-element.28) | copy-start | bytes 4718596
  92.6 1.2 copy-start.23
  93.8 4.5 %copy-start.5 = (bf16[1,2,8,128,384]{4,3,2,1,0:T(8,128)(2,1)S(1)}, bf16[1,2,8,128,384]{4,3,2,1,0:T(8,128)(2,1)}, u32[]{:S(2)}) copy-start(bf16[1,2,8,128,384]{4,3,2,1,0:T(8,128)(2,1)} %get-tuple-element.23) | copy-start | bytes 4718596
  93.8 4.5 %copy-start.6 = (bf16[1,2,8,128,384]{4,3,2,1,0:T(8,128)(2,1)S(1)}, bf16[1,2,8,128,384]{4,3,2,1,0:T(8,128)(2,1)}, u32[]{:S(2)}) copy-start(bf16[1,2,8,128,384]{4,3,2,1,0:T(8,128)(2,1)} %get-tuple-element.24) | copy-start | bytes 4718596
  98.2 1.2 copy-start.22
  99.4 4.6 %copy-start.3 = (bf16[1,2,8,128,384]{4,3,2,1,0:T(8,128)(2,1)S(1)}, bf16[1,2,8,128,384]{4,3,2,1,0:T(8,128)(2,1)}, u32[]{:S(2)}) copy-start(bf16[1,2,8,128,384]{4,3,2,1,0:T(8,128)(2,1)} %get-tuple-element.21) | copy-start | bytes 4718596
  99.4 4.6 %copy-start.4 = (bf16[1,2,8,128,384]{4,3,2,1,0:T(8,128)(2,1)S(1)}, bf16[1,2,8,128,384]{4,3,2,1,0:T(8,128)(2,1)}, u32[]{:S(2)}) copy-start(bf16[1,2,8,128,384]{4,3,2,1,0:T(8,128)(2,1)} %get-tuple-element.22) | copy-start | bytes 4718596
  104.0 1.2 copy-start.21
  105.2 4.5 %copy-start.1 = (bf16[1,2,8,128,384]{4,3,2,1,0:T(8,128)(2,1)S(1)}, bf16[1,2,8,128,384]{4,3,2,1,0:T(8,128)(2,1)}, u32[]{:S(2)}) copy-start(bf16[1,2,8,128,384]{4,3,2,1,0:T(8,128)(2,1)} %get-tuple-element.31) | copy-start | bytes 4718596
  105.2 4.5 %copy-start.2 = (bf16[1,2,8,128,384]{4,3,2,1,0:T(8,128)(2,1)S(1)}, bf16[1,2,8,128,384]{4,3,2,1,0:T(8,128)(2,1)}, u32[]{:S(2)}) copy-start(bf16[1,2,8,128,384]{4,3,2,1,0:T(8,128)(2,1)} %get-tuple-element.32) | copy-start | bytes 4718596
  109.7 3.2 %copy-start.20 = (bf16[1,1,3,384,384]{4,3,2,1,0:T(8,128)(2,1)S(1)}, bf16[1,1,3,384,384]{4,3,2,1,0:T(8,128)(2,1)}, u32[]{:S(2)}) copy-start(bf16[1,1,3,384,384]{4,3,2,1,0:T(8,128)(2,1)} %get-tuple-element.15) | copy-start | bytes 2654212
  112.9 4.5 %copy-start.13 = (bf16[1,2,8,128,1152]{4,3,2,1,0:T(8,128)(2,1)S(1)}, bf16[1,2,8,128,1152]{4,3,2,1,0:T(8,128)(2,1)}, u32[]{:S(2)}) copy-start(bf16[1,2,8,128,1152]{4,3,2,1,0:T(8,128)(2,1)} %get-tuple-element.47) | copy-start | bytes 14155780
  112.9 4.5 %copy-start.19 = (bf16[1,1,3,384,384]{4,3,2,1,0:T(8,128)(2,1)S(1)}, bf16[1,1,3,384,384]{4,3,2,1,0:T(8,128)(2,1)}, u32[]{:S(2)}) copy-start(bf16[1,1,3,384,384]{4,3,2,1,0:T(8,128)(2,1)} %get-tuple-element.12) | copy-start | bytes 2654212
  117.4 4.5 %copy-start.18 = (bf16[1,1,3,384,384]{4,3,2,1,0:T(8,128)(2,1)S(1)}, bf16[1,1,3,384,384]{4,3,2,1,0:T(8,128)(2,1)}, u32[]{:S(2)}) copy-start(bf16[1,1,3,384,384]{4,3,2,1,0:T(8,128)(2,1)} %get-tuple-element.17) | copy-start | bytes 2654212
  121.9 5.2 %copy-start.17 = (f32[2048,384]{1,0:T(8,128)S(1)}, f32[2048,384]{1,0:T(8,128)}, u32[]{:S(2)}) copy-start(f32[2048,384]{1,0:T(8,128)} %fusion.25) | copy-start | bytes 9437188
  126.4 1.2 copy-start.14
  126.4 2.2 %copy-start.15 = (f32[2048,384]{1,0:T(8,128)S(1)}, f32[2048,384]{1,0:T(8,128)}, u32[]{:S(2)}) copy-start(f32[2048,384]{1,0:T(8,128)} %fusion.22) | copy-start | bytes 9437188
  126.4 3.1 %copy-start.16 = (f32[2048,384]{1,0:T(8,128)S(1)}, f32[2048,384]{1,0:T(8,128)}, u32[]{:S(2)}) copy-start(f32[2048,384]{1,0:T(8,128)} %fusion.24) | copy-start | bytes 9437188
  129.5 7.7 %copy-start = (bf16[1,2,8,128,384]{4,3,2,1,0:T(8,128)(2,1)S(1)}, bf16[1,2,8,128,384]{4,3,2,1,0:T(8,128)(2,1)}, u32[]{:S(2)}) copy-start(bf16[1,2,8,128,384]{4,3,2,1,0:T(8,128)(2,1)} %param.5) | copy-start | bytes 4718596
  129.5 7.7 %copy-start.26 = (f32[384]{0:T(512)S(1)}, f32[384]{0:T(512)}, u32[]{:S(2)}) copy-start(f32[384]{0:T(512)} %param.9) | copy-start | bytes 4612
where the time goes:
time: 139 us
  matrix products  43.9 us (32%)
  waiting for transfers between devices  34.7 us (25%)
  local copies, waits for them, and re-layouts  23.1 us (17%)
  other arithmetic  17 us (12%)
  blocking collectives  11.8 us (8%)
  starting transfers between devices  8.32 us (6%)
    dot_general x9, matrix products, convolve(): jnp.dot(columns.reshape(-1, 3 * channels), kernel, preferred_element_type...  43.9 us
    ppermute x1, waiting for transfers between devices, from_behind(): lax.ppermute(value, axis, [(source, source + steps) for source in range(i...  34.7 us
    psum x1, blocking collectives, shards(): lax.psum((grouped(chan_sum, per_group), grouped(chan_raw, per_group)), ('...  11.8 us
    slice x1, local copies, waits for them, and re-layouts, convolve(): slab_rows[:, :, :, 0:width_dev]  10.3 us
    concatenate x7, other arithmetic, convolve(): jnp.concatenate([slab_rows[:, :, :, 0:width_dev], slab_rows[:, :, :, 1:wi...  7.53 us
    slice x1, local copies, waits for them, and re-layouts, convolve(): kernel = conv_weight[tap_time, tap_row].reshape(3 * channels, -1)  5.77 us
    unnamed x54, local copies, waits for them, and re-layouts  5.37 us
    ppermute x1, starting transfers between devices, with_halo(): lax.ppermute(lax.slice_in_dim(block, 0, width, axis=dim), axis, backward)  4.49 us
  transfers between devices with their start and end apart: 3, of which 1 were waited for; matrix products, arithmetic and copies ran while one was open for 4% of the time, Pallas kernels for 0%

commit v1 on v0

v1 whole, which is shorter than its diff:
```python
import functools

import jax
import jax.numpy as jnp
from jax import lax
from jax.experimental import pallas as pl
from jax.experimental.pallas import tpu as pltpu
from jax.sharding import PartitionSpec as P


GROUPS = 32
epsilon = 1e-06
TAPS = 3
BLOCK = 2
MIB = 1024 * 1024


def ring(value, axis, step):
    count = lax.axis_size(axis)
    return lax.ppermute(value, axis, [(i, (i + step) % count) for i in range(count)])


def row_halo(first, last, axis, above):
    count = lax.axis_size(axis)
    if count == 1:
        return first, last
    if count == 2:
        both = ring(jnp.where(above == 0, last, first), axis, 1)
        return both, both
    return ring(last, axis, 1), ring(first, axis, -1)


def merged(stats, axis, step, count):
    size = lax.axis_size(axis)
    other = lax.ppermute(stats, axis, [(i, i ^ step) for i in range(size)])
    gap = stats[0:1] - other[0:1]
    second = lax.broadcasted_iota(jnp.int32, stats.shape, 0) == 1
    return stats + other + jnp.where(second, gap * gap * (0.5 / count), 0.0)


def prep_kernel(flags_ref, x_ref, w_ref, stats_ref, above_ref, keep_ref, w_all_ref, near_ref, edge_ref, far_ref, sems):
    frames, height, width, channels = keep_ref.shape
    fetch = pltpu.make_async_copy(x_ref, keep_ref, sems.at[0])
    fetch.start()
    copies = []
    for i, kt in enumerate((2, 1, 0)):
        copies.append(pltpu.make_async_copy(w_ref.at[kt], w_all_ref.at[:, pl.ds(i * channels, channels)], sems.at[1 + i]))
    for copy in copies:
        copy.start()
    fetch.wait()
    pieces = [
        pltpu.make_async_copy(keep_ref.at[1, pl.ds(1, height - 2)], near_ref, sems.at[4]),
        pltpu.make_async_copy(keep_ref.at[0, 0], edge_ref.at[0], sems.at[5]),
        pltpu.make_async_copy(keep_ref.at[0, height - 1], edge_ref.at[1], sems.at[6]),
        pltpu.make_async_copy(keep_ref.at[0, pl.ds(1, height - 2)], far_ref, sems.at[7]),
    ]
    for copy in pieces:
        copy.start()
    above_ref[...] = jnp.full(above_ref.shape, flags_ref[1], jnp.int32)
    per_step = 8
    steps = frames * height

    def tile(r):
        return keep_ref[r // height, r % height].astype(jnp.float32).reshape(-1, per_step, channels)

    def add(r, total):
        return total + jnp.sum(tile(r), axis=0)

    zeros = jnp.zeros((per_step, channels), jnp.float32)
    chan_sum = jnp.sum(lax.fori_loop(0, steps, add, zeros, unroll=2), axis=0, keepdims=True)
    mean = chan_sum * (1.0 / (steps * width))

    def square(r, total):
        gap = tile(r) - mean
        return total + jnp.sum(gap * gap, axis=0)

    stats_ref[0:1] = chan_sum
    stats_ref[1:2] = jnp.sum(lax.fori_loop(0, steps, square, zeros, unroll=2), axis=0, keepdims=True)
    for copy in copies + pieces:
        copy.wait()


def affine(stats_ref, gain_ref, bias_ref, aff_ref, count):
    channels = stats_ref.shape[-1]
    per_group = channels // GROUPS
    row = lax.broadcasted_iota(jnp.int32, (channels, channels), 0)
    col = lax.broadcasted_iota(jnp.int32, (channels, channels), 1)
    same = jnp.where(row // per_group == col // per_group, 1.0, 0.0)

    def group_mean(v):
        wide = jnp.broadcast_to(v, (8, channels))
        dot = jnp.dot(wide, same, precision=lax.Precision.HIGHEST, preferred_element_type=jnp.float32)
        return dot[0:1] * (1.0 / per_group)

    chan_mean = stats_ref[0:1] * (1.0 / count)
    mean = group_mean(chan_mean)
    gap = chan_mean - mean
    var = group_mean(stats_ref[1:2] * (1.0 / count) + gap * gap)
    aff_ref[0:1] = mean
    aff_ref[1:2] = lax.rsqrt(var + epsilon) * gain_ref[...].reshape(1, channels)
    aff_ref[2:3] = bias_ref[...].reshape(1, channels)


def activate(raw, aff, keep, act_ref, slot):
    width, channels = raw.shape
    normed = (raw.astype(jnp.float32) - aff[0:1]) * aff[1:2] + aff[2:3]
    active = normed * jax.nn.sigmoid(normed)
    if keep is not None:
        active = jnp.where(keep != 0, active, 0.0)
    place = lax.broadcasted_iota(jnp.int32, (width, channels), 0)
    before = jnp.where(place == 0, 0.0, pltpu.roll(active, 1, 0))
    after = jnp.where(place == width - 1, 0.0, pltpu.roll(active, width - 1, 0))
    act_ref[slot, :, 0:channels] = before.astype(jnp.bfloat16)
    act_ref[slot, :, channels : 2 * channels] = active.astype(jnp.bfloat16)
    act_ref[slot, :, 2 * channels : 3 * channels] = after.astype(jnp.bfloat16)


def taps(act_ref, first, rows):
    parts = []
    for kh in range(TAPS):
        part = act_ref[pl.ds(first + kh, rows)]
        parts.append(part.reshape(-1, part.shape[-1]))
    return jnp.concatenate(parts, axis=-1)


def own_kernel(count, flags_ref, x_ref, top_ref, bottom_ref, stats_ref, gain_ref, bias_ref, w_ref,
               acc0_ref, acc1_ref, aff_ref, act0_ref, act1_ref):
    _, height, width, channels = x_ref.shape
    steps = height // BLOCK
    affine(stats_ref, gain_ref, bias_ref, aff_ref, count)
    aff = aff_ref[0:3]

    def fill(f, slot, act_ref):
        if isinstance(slot, int):
            if slot == 0:
                return activate(top_ref[f], aff, flags_ref[1], act_ref, slot)
            if slot == height + 1:
                return activate(bottom_ref[f], aff, flags_ref[2], act_ref, slot)
            return activate(x_ref[f, slot - 1], aff, None, act_ref, slot)
        raw = jnp.where(slot == 0, top_ref[f], x_ref[f, jnp.clip(slot - 1, 0, height - 1)])
        raw = jnp.where(slot == height + 1, bottom_ref[f], raw)
        keep = jnp.where(slot == 0, flags_ref[1], jnp.where(slot == height + 1, flags_ref[2], 1))
        return activate(raw, aff, keep, act_ref, slot)

    for slot in range(BLOCK + 2):
        fill(0, slot, act0_ref)
    per_step = -(-(height + 2) // steps)

    def wide_step(i, _):
        first = i * BLOCK
        both = jnp.dot(taps(act0_ref, first, BLOCK), w_ref[:, 0 : 2 * channels], preferred_element_type=jnp.float32)
        acc0_ref[pl.ds(first, BLOCK)] = both[:, 0:channels].reshape(BLOCK, width, channels)
        acc1_ref[pl.ds(first, BLOCK)] = both[:, channels:].reshape(BLOCK, width, channels)
        for r in range(BLOCK):
            fill(0, jnp.minimum(first + BLOCK + 2 + r, height + 1), act0_ref)
        for r in range(per_step):
            fill(1, jnp.minimum(i * per_step + r, height + 1), act1_ref)
        return 0

    lax.fori_loop(0, steps, wide_step, 0)

    def slim_step(i, _):
        first = i * BLOCK
        last = jnp.dot(taps(act1_ref, first, BLOCK), w_ref[:, 0:channels], preferred_element_type=jnp.float32)
        here = pl.ds(first, BLOCK)
        acc1_ref[here] = acc1_ref[here] + last.reshape(BLOCK, width, channels)
        return 0

    lax.fori_loop(0, steps, slim_step, 0)


def halo_fill(flags_ref, edge_ref, mid_ref, top_ref, bottom_ref, aff, act_ref, slot):
    height = mid_ref.shape[0] + 2
    keep = flags_ref[0]
    if isinstance(slot, int):
        if slot == 0:
            return activate(top_ref[...], aff, keep * flags_ref[1], act_ref, slot)
        if slot == height + 1:
            return activate(bottom_ref[...], aff, keep * flags_ref[2], act_ref, slot)
        if slot == 1 or slot == height:
            return activate(edge_ref[int(slot == height)], aff, keep, act_ref, slot)
        return activate(mid_ref[slot - 2], aff, keep, act_ref, slot)
    raw = jnp.where(slot == height, edge_ref[1], mid_ref[jnp.clip(slot - 2, 0, height - 3)])
    raw = jnp.where(slot == height + 1, bottom_ref[...], raw)
    return activate(raw, aff, keep * jnp.where(slot == height + 1, flags_ref[2], 1), act_ref, slot)


def near_kernel(flags_ref, edge_ref, mid_ref, top_ref, bottom_ref, aff_ref, x_ref, cbias_ref, acc0_ref, acc1_ref, w_ref,
                new0_ref, out_ref, act_ref, line_ref, sems):
    height, width, channels = acc0_ref.shape
    aff = aff_ref[0:3]
    cbias = cbias_ref[...].reshape(1, channels)
    fill = functools.partial(halo_fill, flags_ref, edge_ref, mid_ref, top_ref, bottom_ref, aff, act_ref)
    for slot in range(BLOCK + 2):
        fill(slot)

    def copy_out(i):
        here = pl.ds(i * BLOCK, BLOCK)
        return pltpu.make_async_copy(line_ref.at[here], out_ref.at[1, here], sems.at[i])

    def step(i, _):
        first = i * BLOCK
        both = jnp.dot(taps(act_ref, first, BLOCK), w_ref[:, channels:], preferred_element_type=jnp.float32)
        both = both.reshape(BLOCK, width, 2 * channels)
        here = pl.ds(first, BLOCK)
        new0_ref[here] = acc0_ref[here] + both[:, :, 0:channels]
        done = x_ref[1, here].astype(jnp.float32) + (acc1_ref[here] + both[:, :, channels:]) + cbias
        line_ref[here] = done.astype(jnp.bfloat16)
        for r in range(BLOCK):
            fill(jnp.minimum(first + BLOCK + 2 + r, height + 1))
        copy_out(i).start()
        return 0

    lax.fori_loop(0, height // BLOCK, step, 0)
    for i in range(height // BLOCK):
        copy_out(i).wait()


def far_kernel(flags_ref, edge_ref, mid_ref, top_ref, bottom_ref, aff_ref, x_ref, cbias_ref, acc0_ref, w_ref, old_ref,
               out_ref, act_ref, line_ref, sems):
    del old_ref
    height, width, channels = acc0_ref.shape
    aff = aff_ref[0:3]
    cbias = cbias_ref[...].reshape(1, channels)
    fill = functools.partial(halo_fill, flags_ref, edge_ref, mid_ref, top_ref, bottom_ref, aff, act_ref)
    for slot in range(BLOCK + 2):
        fill(slot)

    def copy_out(i):
        here = pl.ds(i * BLOCK, BLOCK)
        return pltpu.make_async_copy(line_ref.at[here], out_ref.at[0, here], sems.at[i])

    def step(i, _):
        first = i * BLOCK
        part = jnp.dot(taps(act_ref, first, BLOCK), w_ref[:, 2 * channels :], preferred_element_type=jnp.float32)
        here = pl.ds(first, BLOCK)
        done = x_ref[0, here].astype(jnp.float32) + (acc0_ref[here] + part.reshape(BLOCK, width, channels)) + cbias
        line_ref[here] = done.astype(jnp.bfloat16)
        for r in range(BLOCK):
            fill(jnp.minimum(first + BLOCK + 2 + r, height + 1))
        copy_out(i).start()
        return 0

    lax.fori_loop(0, height // BLOCK, step, 0)
    for i in range(height // BLOCK):
        copy_out(i).wait()


def shards(inputs, norm_gain, norm_bias, conv_weight, conv_bias):
    clips, frames, height, width, channels = inputs.shape
    assert clips == 1 and frames == TAPS - 1 and height % BLOCK == 0
    f32, bf16 = jnp.float32, jnp.bfloat16
    x = inputs.reshape(frames, height, width, channels)
    weight = conv_weight.reshape(TAPS, TAPS * TAPS * channels, channels)
    flags = jnp.stack([
        (lax.axis_index("tm") > 0).astype(jnp.int32),
        (lax.axis_index("rows") > 0).astype(jnp.int32),
        (lax.axis_index("rows") < lax.axis_size("rows") - 1).astype(jnp.int32),
    ])
    vmem = pl.BlockSpec(memory_space=pltpu.VMEM)
    smem = pl.BlockSpec(memory_space=pltpu.SMEM)
    hbm = pl.BlockSpec(memory_space=pltpu.HBM)
    shape = jax.ShapeDtypeStruct
    dma = pltpu.SemaphoreType.DMA

    def params(mib):
        return pltpu.CompilerParams(vmem_limit_bytes=mib * MIB)

    near_edge = ring(x[1, :: height - 1], "tm", 1)
    stats, above, kept, w_all, near_src, far_edge_src, far_src = pl.pallas_call(
        prep_kernel,
        out_shape=(
            shape((2, channels), f32), shape((channels,), jnp.int32), pltpu.VMEM(x.shape, bf16),
            pltpu.VMEM((weight.shape[1], TAPS * channels), bf16), shape((height - 2, width, channels), bf16),
            shape((2, width, channels), bf16), shape((height - 2, width, channels), bf16)),
        in_specs=[smem, hbm, hbm], out_specs=(vmem, vmem, vmem, vmem, hbm, hbm, hbm), scratch_shapes=[dma((8,))],
        compiler_params=params(2), name="prep")(
            flags, pltpu.with_memory_space_constraint(x, pltpu.HBM), pltpu.with_memory_space_constraint(weight, pltpu.HBM))

    kept, w_all = (pltpu.with_memory_space_constraint(v, pltpu.VMEM) for v in (kept, w_all))
    count = 1.0 * frames * height * width
    step = 1
    while step < lax.axis_size("rows"):
        stats = merged(stats, "rows", step, count)
        count, step = 2.0 * count, 2 * step
    step = 1
    while step < lax.axis_size("tm"):
        stats = merged(stats, "tm", step, count)
        count, step = 2.0 * count, 2 * step

    own_top, own_bottom = row_halo(x[:, 0], x[:, height - 1], "rows", above)
    near_mid = ring(near_src, "tm", 1)
    far_edge = ring(far_edge_src, "tm", 1)
    far_mid = ring(far_src, "tm", 1)
    near_top, near_bottom = row_halo(near_edge[0], near_edge[1], "rows", above)
    far_top, far_bottom = row_halo(far_edge[0], far_edge[1], "rows", above)

    act = pltpu.VMEM((height + 2, width, TAPS * channels), bf16)
    line = pltpu.VMEM((height, width, channels), bf16)
    acc = pltpu.VMEM((height, width, channels), f32)

    acc0, acc1, aff = pl.pallas_call(
        functools.partial(own_kernel, count),
        out_shape=(acc, acc, pltpu.VMEM((8, channels), f32)),
        in_specs=[smem] + [vmem] * 7, out_specs=(vmem, vmem, vmem),
        scratch_shapes=[act, act],
        compiler_params=params(12), name="own")(
            flags, kept, own_top, own_bottom, stats, norm_gain, norm_bias, w_all)

    acc0, out = pl.pallas_call(
        near_kernel,
        out_shape=(acc, shape((frames, height, width, channels), bf16)),
        in_specs=[smem] + [vmem] * 10, out_specs=(vmem, hbm),
        scratch_shapes=[act, line, dma((height // BLOCK,))],
        compiler_params=params(8), name="near")(
            flags, near_edge, near_mid, near_top, near_bottom, aff, kept, conv_bias, acc0, acc1, w_all)

    out = pl.pallas_call(
        far_kernel,
        out_shape=shape((frames, height, width, channels), bf16),
        in_specs=[smem] + [vmem] * 9 + [hbm], out_specs=hbm,
        scratch_shapes=[act, line, dma((height // BLOCK,))],
        input_output_aliases={10: 0},
        compiler_params=params(8), name="far")(
            flags, far_edge, far_mid, far_top, far_bottom, aff, kept, conv_bias, acc0, w_all, out)
    return out.reshape(inputs.shape)


def solution(mesh):
    placed = (P("batch", "tm", "rows", None, None), P(), P(), P(), P())
    return jax.shard_map(
        shards,
        mesh=mesh,
        in_specs=placed,
        out_specs=P("batch", "tm", "rows", None, None),
        check_vma=False,
    )
```

time: 139 us -> 77.5 us (0.56)
  the two profiles are of different devices: /device:TPU:29 before, /device:TPU:0 now
where the time goes in v1:
time: 77.5 us; the launch traced here: 77.3 us
  Pallas kernels  34.4 us (44%)
  waiting for transfers between devices  31.2 us (40%)
  starting transfers between devices  9.25 us (12%)
  other arithmetic  1.46 us (2%)
  local copies, waits for them, and re-layouts  0.96 us (1%)
    ppermute x3, waiting for transfers between devices, merged(): other = lax.ppermute(stats, axis, [(i, i ^ step) for i in range(size)])  30.5 us
    pallas_call x1, Pallas kernels, shards(): pl.pallas_call(functools.partial(own_kernel, count), out_shape=(acc, acc,...  14.3 us
    pallas_call x1, Pallas kernels, shards(): pl.pallas_call(near_kernel, out_shape=(acc, shape((frames, height, width,...  8.91 us
    ppermute x7, starting transfers between devices, ring(): lax.ppermute(value, axis, [(i, (i + step) % count) for i in range(count)])  6.77 us
    pallas_call x1, Pallas kernels, shards(): pl.pallas_call(far_kernel, out_shape=shape((frames, height, width, channe...  6.77 us
    pallas_call x1, Pallas kernels, shards(): pl.pallas_call(prep_kernel, out_shape=(shape((2, channels), f32), shape((...  4.41 us
    ppermute x3, starting transfers between devices, merged(): other = lax.ppermute(stats, axis, [(i, i ^ step) for i in range(size)])  2.48 us
  transfers between devices with their start and end apart: 10, of which 3 were waited for; matrix products, arithmetic and copies ran while one was open for 2% of the time, Pallas kernels for 36%

profile of v1, /device:TPU:0, one launch (start us, length us, event | category | flops | bytes accessed | tf_op | source)
XLA Modules:
  0.0 77.3 jit_solution(14813163240186604587)
XLA Ops:
  0.0 0.9 %slice_bitcast_fusion.2 = bf16[2,128,384]{2,1,0:T(8,128)(2,1)S(1)} fusion(bf16[2,8,128,384]{3,2,1,0:T(8,128)(2,1)} %bitcast.35), kind=kLoop, calls=%fused_computation.3 | loop fusion | bytes 393216 | tf_op jit(solution)/shard_map/squeeze | solution.py:269
  1.0 3.0 %collective-permute-start.7 = (bf16[2,128,384]{2,1,0:T(8,128)(2,1)S(1)}, bf16[2,128,384]{2,1,0:T(8,128)(2,1)S(1)}, u32[]{:S(2)}, u32[]{:S(2)}) collective-permute-start(bf16[2,128,384]{2,1,0:T(8,128)(2,1)S(1)} %slice_bitcast_fusion.2), channel_id=1, source_target_pairs={{0,8},{8,16},{16,24},{24,0},{1,9},{9,17},{17,25},{25,1},{2,10},{10... | collective-permute-start | bytes 589832 | tf_op jit(solution)/shard_map/ppermute | solution.py:20
  4.0 0.1 add_convert_fusion.flags_ref
  4.0 0.0 copy-start.1
  4.0 0.0 copy-start.2
  4.1 4.4 %prep.1 = (f32[2,384]{1,0:T(2,128)S(1)}, s32[384]{0:T(512)S(1)}, bf16[2,8,128,384]{3,2,1,0:T(8,128)(2,1)S(1)}, bf16[3456,1152]{1,0:T(8,128)(2,1)S(1)}, bf16[6,12...) custom-call(s32[3]{0:T(128)S(1)} %add_convert_fusion.flags_ref, ...), custom_call_target="tpu_custom_call" | custom-call | tf_op jit(solution)/shard_map/prep/pallas_call | solution.py:270
  8.5 0.1 collective-permute-start.4
  8.5 1.5 %collective-permute-start = (bf16[2,128,384]{2,1,0:T(8,128)(2,1)S(1)}, bf16[2,128,384]{2,1,0:T(8,128)(2,1)S(1)}, u32[]{:S(2)}, u32[]{:S(2)}) collective-permute-start(bf16[2,128,384]{2,1,0:T(8,128)(2,1)S(1)} %get-tuple-element.17), channel_id=1, source_target_pairs={{0,8},{8,16},{16,24},{24,0},{1,9},{9,17},{17,25},{25,1},{2,10},{10... | collective-permute-start | bytes 589832 | tf_op jit(solution)/shard_map/ppermute | solution.py:20
  10.1 1.5 %collective-permute-start.1 = (bf16[6,128,384]{2,1,0:T(8,128)(2,1)S(1)}, bf16[6,128,384]{2,1,0:T(8,128)(2,1)S(1)}, u32[]{:S(2)}, u32[]{:S(2)}) collective-permute-start(bf16[6,128,384]{2,1,0:T(8,128)(2,1)S(1)} %get-tuple-element.18), channel_id=1, source_target_pairs={{0,8},{8,16},{16,24},{24,0},{1,9},{9,17},{17,25},{25,1},{2,10},{10... | collective-permute-start | bytes 1769480 | tf_op jit(solution)/shard_map/ppermute | solution.py:20
  11.6 0.1 collective-permute-start.8
  11.7 0.0 collective-permute-done.4
  11.7 0.1 select_add_fusion.2
  11.8 1.9 %collective-permute-start.5 = (f32[2,384]{1,0:T(2,128)S(1)}, f32[2,384]{1,0:T(2,128)S(1)}, u32[]{:S(2)}, u32[]{:S(2)}) collective-permute-start(f32[2,384]{1,0:T(2,128)S(1)} %select_add_fusion.2), channel_id=1, source_target_pairs={{0,8},{8,0},{16,24},{24,16},{1,9},{9,1},{17,25},{25,17},{2,10},{10... | collective-permute-start | bytes 9224 | tf_op jit(solution)/shard_map/ppermute | solution.py:35
  13.7 28.5 %collective-permute-done.5 = f32[2,384]{1,0:T(2,128)S(1)} collective-permute-done((f32[2,384]{1,0:T(2,128)S(1)}, f32[2,384]{1,0:T(2,128)S(1)}, u32[]{:S(2)}, u32[]{:S(2)}) %collective-permute-start.5) | collective-permute-done | bytes 3104 | tf_op jit(solution)/shard_map/ppermute | solution.py:35
  42.2 0.1 select_add_fusion.1
  42.3 0.5 collective-permute-start.6
  42.8 1.0 %fusion = bf16[2,128,384]{2,1,0:T(8,128)(2,1)S(1)} fusion(bf16[2,8,128,384]{3,2,1,0:T(8,128)(2,1)} %bitcast.37, pred[384]{0:T(512)(128)(4,1)S(1)} %broadcast_compare_fusion), kind=kLoop, calls=%fused_computation.1 | loop fusion | flops 98304 | bytes 590208 | tf_op jit(solution)/shard_map/jit(_where)/select_n | solution.py:28
  43.8 2.0 %collective-permute-done.6 = f32[2,384]{1,0:T(2,128)S(1)} collective-permute-done((f32[2,384]{1,0:T(2,128)S(1)}, f32[2,384]{1,0:T(2,128)S(1)}, u32[]{:S(2)}, u32[]{:S(2)}) %collective-permute-start.6) | collective-permute-done | bytes 3104 | tf_op jit(solution)/shard_map/ppermute | solution.py:35
  45.8 0.0 collective-permute-start.3
  45.9 0.0 collective-permute-done.7.edge_ref
  45.9 0.0 collective-permute-done.edge_ref
  45.9 0.6 collective-permute-start.9
  46.5 0.1 collective-permute-start.2
  46.6 0.1 select_add_fusion.stats_ref
  46.7 0.6 collective-permute-done.3.top_ref.bottom_ref
  47.3 0.0 copy-done.1
  47.3 0.0 copy-done.2
  47.3 0.0 copy-start
  47.3 14.3 %own.1 = (f32[8,128,384]{2,1,0:T(8,128)S(1)}, f32[8,128,384]{2,1,0:T(8,128)S(1)}, f32[8,384]{1,0:T(8,128)S(1)}) custom-call(s32[3]{0:T(128)S(1)} %add_convert_fusion.flags_ref, bf16[2,8,128,384]{3,2,1,0:T(8,128)(2,1)S(1)} %get-tuple-element.20.x_ref, bf16[2,128,384]{2,1,0:T(8,128)(2,1)S(1)} %collective-permute-done.3.top_ref.bottom_ref, ...), custom_call_target="tpu_custom_call" | custom-call | tf_op jit(solution)/shard_map/own/pallas_call | solution.py:302
  61.6 0.0 collective-permute-done.9.top_ref.bottom_ref
  61.6 0.0 collective-permute-done.8.mid_ref
  61.6 0.0 copy-done
  61.6 8.9 %near.1 = (f32[8,128,384]{2,1,0:T(8,128)S(1)}, bf16[2,8,128,384]{3,2,1,0:T(8,128)(2,1)}) custom-call(s32[3]{0:T(128)S(1)} %add_convert_fusion.flags_ref, bf16[2,128,384]{2,1,0:T(8,128)(2,1)S(1)} %collective-permute-done.7.edge_ref, bf16[6,128,384]{2,1,0:T(8,128)(2,1)S(1)} %collective-permute-done.8.mid_ref, ...), custom_call_target="tpu_custom_call" | custom-call | tf_op jit(solution)/shard_map/near/pallas_call | solution.py:310
  70.6 0.0 collective-permute-done.2.top_ref.bottom_ref
  70.6 0.0 collective-permute-done.1.mid_ref
  70.6 6.8 %far.1 = bf16[2,8,128,384]{3,2,1,0:T(8,128)(2,1)} custom-call(s32[3]{0:T(128)S(1)} %add_convert_fusion.flags_ref, bf16[2,128,384]{2,1,0:T(8,128)(2,1)S(1)} %collective-permute-done.edge_ref, bf16[6,128,384]{2,1,0:T(8,128)(2,1)S(1)} %collective-permute-done.1.mid_ref, ...), custom_call_target="tpu_custom_call", output_to_operand_aliasing={{}: (10, {})} | custom-call | tf_op jit(solution)/shard_map/far/pallas_call | solution.py:318
  (6 shorter events, 0.1 us)
Async XLA Ops:
  1.0 44.9 %collective-permute-start.7 = (bf16[2,128,384]{2,1,0:T(8,128)(2,1)S(1)}, bf16[2,128,384]{2,1,0:T(8,128)(2,1)S(1)}, u32[]{:S(2)}, u32[]{:S(2)}) collective-permute-start(bf16[2,128,384]{2,1,0:T(8,128)(2,1)S(1)} %slice_bitcast_fusion.2), channel_id=1, source_target_pairs={{0,8},{8,16},{16,24},{24,0},{1,9},{9,17},{17,25},{25,1},{2,10},{10... | collective-permute-start | bytes 589832 | tf_op jit(solution)/shard_map/ppermute | solution.py:20
  4.0 43.2 %copy-start.1 = (f32[384]{0:T(512)S(1)}, f32[384]{0:T(512)}, u32[]{:S(2)}) copy-start(f32[384]{0:T(512)} %gain_ref.1) | copy-start | bytes 4612
  4.0 43.2 %copy-start.2 = (f32[384]{0:T(512)S(1)}, f32[384]{0:T(512)}, u32[]{:S(2)}) copy-start(f32[384]{0:T(512)} %bias_ref.1) | copy-start | bytes 4612
  8.5 3.2 %collective-permute-start.4 = (f32[2,384]{1,0:T(2,128)S(1)}, f32[2,384]{1,0:T(2,128)S(1)}, u32[]{:S(2)}, u32[]{:S(2)}) collective-permute-start(f32[2,384]{1,0:T(2,128)S(1)} %get-tuple-element.21), channel_id=1, source_target_pairs={{0,4},{4,0},{1,5},{5,1},{2,6},{6,2},{3,7},{7,3},{8,12},{12,8},{9,1... | collective-permute-start | bytes 9224 | tf_op jit(solution)/shard_map/ppermute | solution.py:35
  8.5 37.3 %collective-permute-start = (bf16[2,128,384]{2,1,0:T(8,128)(2,1)S(1)}, bf16[2,128,384]{2,1,0:T(8,128)(2,1)S(1)}, u32[]{:S(2)}, u32[]{:S(2)}) collective-permute-start(bf16[2,128,384]{2,1,0:T(8,128)(2,1)S(1)} %get-tuple-element.17), channel_id=1, source_target_pairs={{0,8},{8,16},{16,24},{24,0},{1,9},{9,17},{17,25},{25,1},{2,10},{10... | collective-permute-start | bytes 589832 | tf_op jit(solution)/shard_map/ppermute | solution.py:20
  10.1 60.5 %collective-permute-start.1 = (bf16[6,128,384]{2,1,0:T(8,128)(2,1)S(1)}, bf16[6,128,384]{2,1,0:T(8,128)(2,1)S(1)}, u32[]{:S(2)}, u32[]{:S(2)}) collective-permute-start(bf16[6,128,384]{2,1,0:T(8,128)(2,1)S(1)} %get-tuple-element.18), channel_id=1, source_target_pairs={{0,8},{8,16},{16,24},{24,0},{1,9},{9,17},{17,25},{25,1},{2,10},{10... | collective-permute-start | bytes 1769480 | tf_op jit(solution)/shard_map/ppermute | solution.py:20
  11.6 50.0 %collective-permute-start.8 = (bf16[6,128,384]{2,1,0:T(8,128)(2,1)S(1)}, bf16[6,128,384]{2,1,0:T(8,128)(2,1)S(1)}, u32[]{:S(2)}, u32[]{:S(2)}) collective-permute-start(bf16[6,128,384]{2,1,0:T(8,128)(2,1)S(1)} %get-tuple-element.24), channel_id=1, source_target_pairs={{0,8},{8,16},{16,24},{24,0},{1,9},{9,17},{17,25},{25,1},{2,10},{10... | collective-permute-start | bytes 1769480 | tf_op jit(solution)/shard_map/ppermute | solution.py:20
  11.8 30.4 %collective-permute-start.5 = (f32[2,384]{1,0:T(2,128)S(1)}, f32[2,384]{1,0:T(2,128)S(1)}, u32[]{:S(2)}, u32[]{:S(2)}) collective-permute-start(f32[2,384]{1,0:T(2,128)S(1)} %select_add_fusion.2), channel_id=1, source_target_pairs={{0,8},{8,0},{16,24},{24,16},{1,9},{9,1},{17,25},{25,17},{2,10},{10... | collective-permute-start | bytes 9224 | tf_op jit(solution)/shard_map/ppermute | solution.py:35
  42.3 3.6 %collective-permute-start.6 = (f32[2,384]{1,0:T(2,128)S(1)}, f32[2,384]{1,0:T(2,128)S(1)}, u32[]{:S(2)}, u32[]{:S(2)}) collective-permute-start(f32[2,384]{1,0:T(2,128)S(1)} %select_add_fusion.1), channel_id=1, source_target_pairs={{0,16},{8,24},{16,0},{24,8},{1,17},{9,25},{17,1},{25,9},{2,18},{10... | collective-permute-start | bytes 9224 | tf_op jit(solution)/shard_map/ppermute | solution.py:35
  45.8 1.4 %collective-permute-start.3 = (bf16[2,128,384]{2,1,0:T(8,128)(2,1)S(1)}, bf16[2,128,384]{2,1,0:T(8,128)(2,1)S(1)}, u32[]{:S(2)}, u32[]{:S(2)}) collective-permute-start(bf16[2,128,384]{2,1,0:T(8,128)(2,1)S(1)} %fusion), channel_id=1, source_target_pairs={{0,4},{4,0},{1,5},{5,1},{2,6},{6,2},{3,7},{7,3},{8,12},{12,8},{9,1... | collective-permute-start | bytes 589832 | tf_op jit(solution)/shard_map/ppermute | solution.py:20
  45.9 15.7 %collective-permute-start.9 = (bf16[128,384]{1,0:T(8,128)(2,1)S(1)}, bf16[128,384]{1,0:T(8,128)(2,1)S(1)}, u32[]{:S(2)}, u32[]{:S(2)}) collective-permute-start(bf16[128,384]{1,0:T(8,128)(2,1)S(1)} %get-tuple-element.29), channel_id=1, source_target_pairs={{0,4},{4,0},{1,5},{5,1},{2,6},{6,2},{3,7},{7,3},{8,12},{12,8},{9,1... | collective-permute-start | bytes 294920 | tf_op jit(solution)/shard_map/ppermute | solution.py:20
  46.5 24.1 %collective-permute-start.2 = (bf16[128,384]{1,0:T(8,128)(2,1)S(1)}, bf16[128,384]{1,0:T(8,128)(2,1)S(1)}, u32[]{:S(2)}, u32[]{:S(2)}) collective-permute-start(bf16[128,384]{1,0:T(8,128)(2,1)S(1)} %get-tuple-element.30), channel_id=1, source_target_pairs={{0,4},{4,0},{1,5},{5,1},{2,6},{6,2},{3,7},{7,3},{8,12},{12,8},{9,1... | collective-permute-start | bytes 294920 | tf_op jit(solution)/shard_map/ppermute | solution.py:20
  47.3 14.3 %copy-start = (f32[384]{0:T(512)S(1)}, f32[384]{0:T(512)}, u32[]{:S(2)}) copy-start(f32[384]{0:T(512)} %cbias_ref.3) | copy-start | bytes 4612
